TPU v7x, 32 devices: a whole 2x2x4 slice. The times are simulated.
32 devices in a mesh: expert: 4 (over y, x), tensor: 4 (over z), rep: 2 (over core).
Axes of the slice: x: 2, y: 2, z: 4, core: 2. Of those that a mesh axis runs over, the one named last changes fastest.
Arguments:
- requests: bfloat16 [512, 1536], P('expert', ('tensor', 'rep')), may hold values from -6 to 6
- expert_ids: int32 [512, 2], P('expert'), may hold values from 0 to 3, all different within a row; in each aligned block of 128 rows (0 to 127, 128 to 255, ...) at most 96 rows name the same one
- gate_values: float32 [512, 2], P('expert'), may hold values from 0.2 to 1
- w_up: bfloat16 [4, 1536, 6144], P(None, 'expert', ('tensor', 'rep')), may hold values from -0.15625 to 0.15625
- w_down: bfloat16 [4, 1536, 6144], P(None, 'expert', ('tensor', 'rep')), may hold values from -0.078125 to 0.078125
- tower_in: bfloat16 [1536, 768], P(('tensor', 'rep')), may hold values from -0.15625 to 0.15625
- tower_bias: float32 [768], replicated, may hold values from -3 to 3
- tower_out: float32 [3, 256], replicated, may hold values from -0.375 to 0.375
- out_bias: float32 [3], replicated, may hold values from -3 to 3
Outputs:
- mixed: bfloat16 [512, 1536], P('expert', ('tensor', 'rep'))
- scores: float32 [3, 512], P(None, ('expert', 'tensor', 'rep'))
Inputs may be any that keep to these rules, and one draw needn't show every extreme that they name: `expert_ids`: each row names two different experts. In the rows of one device (128 requests) no expert is named more than 96 times, a bound that some block reaches.
All inputs are finite; a program needn't handle non-finite values.
Results may differ from a plain program's by a relative error of at most 0.015.
Values may be sent and summed in bfloat16 or wider, within the bound.
A program may use at most 64 MiB of HBM per device.

v0:
```python
import jax
import jax.numpy as jnp
from jax import lax
from jax.sharding import PartitionSpec as P


def tower_head(pre, tower_bias, tower_out, out_bias):
    active = jax.nn.relu(pre + tower_bias[None, :])
    active = active.reshape(pre.shape[0], tower_out.shape[0], tower_out.shape[1])
    logits = jnp.sum(active * tower_out[None, :, :], axis=2) + out_bias[None, :]
    return jax.nn.sigmoid(logits).T


def per_device(
    requests, expert_ids, gate_values, w_up, w_down, tower_in, tower_bias, tower_out, out_bias
):
    groups = lax.axis_size("expert")
    experts = w_up.shape[0]
    local_experts = experts // groups
    tok_rows = requests.shape[0]
    capacity = 3 * tok_rows // experts
    serve_up, serve_down = (
        lax.all_to_all(w_up, "expert", split_axis=0, concat_axis=1, tiled=True),
        lax.all_to_all(w_down, "expert", split_axis=0, concat_axis=1, tiled=True),
    )
    flat_ids = expert_ids.reshape(-1)
    onehot = (flat_ids[:, None] == jnp.arange(experts, dtype=jnp.int32)[None, :]).astype(jnp.int32)
    before = jnp.cumsum(onehot, axis=0) - onehot
    slot_rank = jnp.sum(before * onehot, axis=1)
    slots = (flat_ids * capacity + slot_rank).reshape(tok_rows, 2)
    slot_index = jnp.arange(experts * capacity, dtype=jnp.int32)
    spread = (
        (slot_index[:, None] == slots[None, :, 0]) | (slot_index[:, None] == slots[None, :, 1])
    ).astype(jnp.bfloat16)
    full_rows = lax.all_gather(requests, ("tensor", "rep"), axis=1, tiled=True)
    outgoing = jnp.dot(spread, full_rows, preferred_element_type=jnp.float32).astype(jnp.bfloat16)
    incoming = lax.all_to_all(outgoing, "expert", split_axis=0, concat_axis=0, tiled=True)
    shaped = incoming.reshape(groups, local_experts, capacity, incoming.shape[1])
    hidden_pre = jnp.einsum("secd,edh->sech", shaped, serve_up, preferred_element_type=jnp.float32)
    hidden = jax.nn.relu(hidden_pre).astype(jnp.bfloat16)
    partial_value = jnp.einsum(
        "sech,edh->secd", hidden, serve_down, preferred_element_type=jnp.float32
    )
    summed = lax.psum_scatter(
        partial_value.astype(jnp.bfloat16), ("tensor", "rep"), scatter_dimension=3, tiled=True
    ).astype(jnp.float32)
    expert_out = summed.astype(jnp.bfloat16).reshape(
        groups * local_experts * capacity, summed.shape[3]
    )
    returned = lax.all_to_all(expert_out, "expert", split_axis=0, concat_axis=0, tiled=True)
    pick_first = (slots[:, 0:1] == slot_index[None, :]).astype(jnp.bfloat16)
    pick_second = (slots[:, 1:2] == slot_index[None, :]).astype(jnp.bfloat16)
    first = jnp.dot(pick_first, returned, preferred_element_type=jnp.float32)
    second = jnp.dot(pick_second, returned, preferred_element_type=jnp.float32)
    mixed = (gate_values[:, 0:1] * first + gate_values[:, 1:2] * second).astype(jnp.bfloat16)
    pre = lax.psum_scatter(
        jnp.dot(mixed, tower_in, preferred_element_type=jnp.float32).astype(jnp.bfloat16),
        ("tensor", "rep"),
        scatter_dimension=0,
        tiled=True,
    ).astype(jnp.float32)
    scores = tower_head(pre, tower_bias, tower_out, out_bias)
    return (mixed, scores)


def solution(mesh):
    in_specs = (
        P("expert", ("tensor", "rep")),
        P("expert", None),
        P("expert", None),
        P(None, "expert", ("tensor", "rep")),
        P(None, "expert", ("tensor", "rep")),
        P(("tensor", "rep"), None),
        P(),
        P(),
        P(),
    )
    out_specs = (P("expert", ("tensor", "rep")), P(None, ("expert", "tensor", "rep")))
    return jax.shard_map(
        per_device, mesh=mesh, in_specs=in_specs, out_specs=out_specs, check_vma=False
    )
```

profile of v0, /device:TPU:0, one launch (start us, length us, event | category | flops | bytes accessed | tf_op | source)
XLA Modules:
  0.0 198.6 jit_solution(8744839714044765721)
XLA Ops:
  7.2 0.0 reduce-scatter.7.cloned.1.call-start
  7.2 0.8 copy.32
  8.0 0.1 eq.85
  8.2 0.1 eq.81
  8.3 1.2 reduce-window.6
  9.6 0.1 slice.26
  9.6 0.1 copy.34
  9.8 0.1 copy.35
  9.9 0.1 add_bitcast_fusion
  10.0 0.1 reduce_sum.21
  10.1 0.1 copy.36
  10.2 0.7 multiply_add_fusion
  10.9 16.4 %all_gather.3 = bf16[128,1536]{0,1:T(8,128)(2,1)S(1)} all-gather(bf16[128,192]{0,1:T(8,128)(2,1)} %param.9), channel_id=1, replica_groups=mesh['expert'=4,'tensor'=4,'rep'=2] {'tensor','rep'}, dimensions={1}, use_global_device_ids=true | all-gather | bytes 442368 | tf_op jit(solution)/shard_map/all_gather | solution.py:35
  27.3 0.5 convolution_convert_fusion
  27.8 19.8 %all_to_all.39 = bf16[4,96,1536]{2,1,0:T(8,128)(2,1)} all-to-all(bf16[4,96,1536]{2,1,0:T(8,128)(2,1)S(1)} %bitcast.56), channel_id=1, replica_groups=mesh['expert'=4,'tensor'=4,'rep'=2] {'expert'}, dimensions={0} | all-to-all | bytes 2359296 | tf_op jit(solution)/shard_map/all_to_all | solution.py:37
  47.6 30.1 %all_to_all.40 = bf16[4,384,768]{2,1,0:T(8,128)(2,1)S(1)} all-to-all(bf16[4,384,768]{2,1,0:T(8,128)(2,1)S(1)} %copy-done.1), channel_id=1, replica_groups=mesh['expert'=4,'tensor'=4,'rep'=2] {'expert'}, dimensions={0} | all-to-all | bytes 4718592 | tf_op jit(solution)/shard_map/all_to_all | solution.py:23
  77.7 29.5 %all_to_all.41 = bf16[4,384,768]{2,1,0:T(8,128)(2,1)} all-to-all(bf16[4,384,768]{2,1,0:T(8,128)(2,1)S(1)} %copy-done.2), channel_id=1, replica_groups=mesh['expert'=4,'tensor'=4,'rep'=2] {'expert'}, dimensions={0} | all-to-all | bytes 4718592 | tf_op jit(solution)/shard_map/all_to_all | solution.py:24
  107.3 5.5 %fusion = bf16[4,1,96,1536]{3,2,0,1:T(8,128)(2,1)} fusion(bf16[1536,768,1]{1,0,2:T(8,128)(2,1)} %bitcast.58, bf16[4,96,1536]{2,1,0:T(8,128)(2,1)} %all_to_all.39, bf16[1536,768,1]{1,0,2:T(8,128)(2,1)S(1)} %bitcast.57), kind=kOutput, calls=%fused_computation.2 | convolution fusion | flops 1813118976 | bytes 7077888 | tf_op jit(solution)/shard_map/sech,edh->secd/dot_general | solution.py:41
  112.7 2.6 %copy.38 = bf16[4,1,96,1536]{2,0,1,3:T(4,128)(2,1)S(1)} copy(bf16[4,1,96,1536]{3,2,0,1:T(8,128)(2,1)} %fusion) | data formatting | bytes 2359296
  115.4 1.9 reshape.69
  117.3 32.7 %reduce-scatter.7.cloned.1.call-done = bf16[192,384]{1,0:T(8,128)(2,1)} async-done(((bf16[1536,384]{1,0:T(8,128)(2,1)}), bf16[192,384]{1,0:T(8,128)(2,1)}) %reduce-scatter.7.cloned.1.call-update) | async-done | bytes 147472
  150.0 1.1 reshape.70
  151.0 0.8 copy.39
  151.9 3.6 %all-to-all-start.3 = ((bf16[4,96,192]{2,1,0:T(8,128)(2,1)}), bf16[4,96,192]{2,1,0:T(8,128)(2,1)S(1)}, u32[]{:S(2)}, u32[]{:S(2)}) async-start(bf16[4,96,192]{2,1,0:T(8,128)(2,1)} %bitcast.13), calls=%async_computation.3 | async-start | bytes 393216 | tf_op jit(solution)/shard_map/all_to_all | solution.py:50
  155.5 5.2 %all-to-all-done.3 = bf16[4,96,192]{2,1,0:T(8,128)(2,1)S(1)} async-done(((bf16[4,96,192]{2,1,0:T(8,128)(2,1)}), bf16[4,96,192]{2,1,0:T(8,128)(2,1)S(1)}, u32[]{:S(2)}, u32[]{:S(2)}) %all-to-all-start.3) | async-done | bytes 147488 | tf_op jit(solution)/shard_map/all_to_all | solution.py:50
  160.7 0.3 convolution_multiply_fusion
  161.0 0.3 fusion.3
  161.3 0.9 convolution_convert_fusion.2
  162.2 27.9 %reduce-scatter.5.cloned.1.call-done = bf16[16,768]{1,0:T(8,128)(2,1)} async-done(((bf16[128,768]{1,0:T(8,128)(2,1)}), bf16[16,768]{1,0:T(8,128)(2,1)}) %reduce-scatter.5.cloned.1.call-update) | async-done | bytes 24592 | tf_op jit(solution)/shard_map/reduce_scatter | solution.py:56
  190.2 0.7 add_maximum_fusion
  191.0 0.1 multiply_reduce_fusion
  191.1 0.7 copy.37
  (27 shorter events, 0.2 us)
Async XLA Ops:
  7.2 154.1 %copy-start = (bf16[192,768]{1,0:T(8,128)(2,1)S(1)}, bf16[192,768]{1,0:T(8,128)(2,1)}, u32[]{:S(2)}) copy-start(bf16[192,768]{1,0:T(8,128)(2,1)} %param.14) | copy-start | bytes 884740
  7.2 142.8 %reduce-scatter.7.cloned.1.call-start = ((), (), s32[]{:S(2)}) async-start(), calls=%async_computation.7 | async-start | bytes 1327104
  27.8 19.8 %copy-start.1 = (bf16[4,384,768]{2,1,0:T(8,128)(2,1)S(1)}, bf16[4,384,768]{2,1,0:T(8,128)(2,1)}, u32[]{:S(2)}) copy-start(bf16[4,384,768]{2,1,0:T(8,128)(2,1)} %param.12) | copy-start | bytes 7077892
  47.6 30.1 %copy-start.2 = (bf16[4,384,768]{2,1,0:T(8,128)(2,1)S(1)}, bf16[4,384,768]{2,1,0:T(8,128)(2,1)}, u32[]{:S(2)}) copy-start(bf16[4,384,768]{2,1,0:T(8,128)(2,1)} %param.13) | copy-start | bytes 7077892
  117.3 38.2 %copy-start.6 = (f32[128,2]{0,1:T(2,128)S(1)}, f32[128,2]{0,1:T(2,128)}, u32[]{:S(2)}) copy-start(f32[128,2]{0,1:T(2,128)} %param.11) | copy-start | bytes 3076
  117.3 72.9 %copy-start.4 = (f32[768]{0:T(1024)S(1)}, f32[768]{0:T(1024)}, u32[]{:S(2)}) copy-start(f32[768]{0:T(1024)} %param.15) | copy-start | bytes 9220
  117.3 73.7 %copy-start.5 = (f32[3,256]{1,0:T(4,128)S(1)}, f32[3,256]{1,0:T(4,128)}, u32[]{:S(2)}) copy-start(f32[3,256]{1,0:T(4,128)} %param.16) | copy-start | bytes 9220
  117.3 73.7 %copy-start.7 = (f32[3]{0:T(128)S(1)}, f32[3]{0:T(128)}, u32[]{:S(2)}) copy-start(f32[3]{0:T(128)} %param.17) | copy-start | bytes 40
  151.9 8.8 %all-to-all-start.3 = ((bf16[4,96,192]{2,1,0:T(8,128)(2,1)}), bf16[4,96,192]{2,1,0:T(8,128)(2,1)S(1)}, u32[]{:S(2)}, u32[]{:S(2)}) async-start(bf16[4,96,192]{2,1,0:T(8,128)(2,1)} %bitcast.13), calls=%async_computation.3 | async-start | bytes 393216 | tf_op jit(solution)/shard_map/all_to_all | solution.py:50
  155.5 34.7 %reduce-scatter.5.cloned.1.call-start = ((), (), s32[]{:S(2)}) async-start(), calls=%async_computation.6 | async-start | bytes 221184 | tf_op jit(solution)/shard_map/reduce_scatter | solution.py:56
  161.3 30.5 %copy-start.3 = (bf16[128,192]{0,1:T(8,128)(2,1)}, bf16[128,192]{0,1:T(8,128)(2,1)S(1)}, u32[]{:S(2)}) copy-start(bf16[128,192]{0,1:T(8,128)(2,1)S(1)} %fusion.3) | copy-start | bytes 147460
Sparse Core Ops, SparseCore 0:
  117.4 32.5 reduce-scatter.6
  162.4 27.7 reduce-scatter.4
where the time goes:
time: 199 us
  blocking collectives  95.8 us (48%)
  waiting for transfers between devices  65.8 us (33%)
  between operations  14.2 us (7%)
  local copies, waits for them, and re-layouts  8.73 us (4%)
  matrix products  7.42 us (4%)
  starting transfers between devices  3.68 us (2%)
  other arithmetic  2.92 us (1%)
    unnamed x3, waiting for transfers between devices  32.7 us
    all_to_all x1, blocking collectives, per_device(): lax.all_to_all(w_up, 'expert', split_axis=0, concat_axis=1, tiled=True)  30.1 us
    all_to_all x1, blocking collectives, per_device(): lax.all_to_all(w_down, 'expert', split_axis=0, concat_axis=1, tiled=True)  29.5 us
    reduce_scatter x1, waiting for transfers between devices, per_device(): lax.psum_scatter(jnp.dot(mixed, tower_in, preferred_element_type=jnp.floa...  27.9 us
    all_to_all x1, blocking collectives, per_device(): lax.all_to_all(outgoing, 'expert', split_axis=0, concat_axis=0, tiled=True)  19.8 us
    all_gather x1, blocking collectives, per_device(): full_rows = lax.all_gather(requests, ('tensor', 'rep'), axis=1, tiled=True)  16.4 us
    unnamed x22, local copies, waits for them, and re-layouts  7.94 us
    dot_general x1, matrix products, per_device(): jnp.einsum('sech,edh->secd', hidden, serve_down, preferred_element_type=j...  5.47 us
  transfers between devices with their start and end apart: 3, of which 3 were waited for; matrix products, arithmetic and copies ran while one was open for 0% of the time, Pallas kernels for 0%

commit v1 on v0

--- a/solution.py
+++ b/solution.py
@@ -1,7 +1,295 @@
+import functools
 import jax
 import jax.numpy as jnp
 from jax import lax
+from jax.experimental import pallas as pl
+from jax.experimental.pallas import tpu as pltpu
 from jax.sharding import PartitionSpec as P
+
+MESH = pl.DeviceIdType.MESH
+CHUNKS = 2
+F32 = jnp.float32
+BF16 = jnp.bfloat16
+
+
+def stay_kernel(
+    dims, req_ref, meta_ref, up_hbm, down_hbm, tin_hbm, bias_ref, tout_ref, ob_ref,
+    mixed_ref, scores_ref,
+    up, down, tin, ag, meta, xin, xs, hp, r1, s2, r2, hid, mine, dsend0, drecv0, dsend, drecv,
+    fsend, frecv, lsem, ag_s, ag_r, me_s, me_r, x_s, x_r, s1_s, s1_r, s2_s, s2_r, h_s, h_r,
+    p_s, p_r, d_s, d_r, f_s, f_r,
+):
+    nx, nt, nr, experts, tok, feat, hcols, tasks, th = dims
+    xe, t, r = lax.axis_index("expert"), lax.axis_index("tensor"), lax.axis_index("rep")
+    sub = tok // CHUNKS
+    started = []
+
+    def remote(src, dst, ssem, rsem, dev):
+        return pltpu.make_async_remote_copy(
+            src_ref=src, dst_ref=dst, send_sem=ssem, recv_sem=rsem, device_id=dev,
+            device_id_type=MESH)
+
+    def send(src, dst, ssem, rsem, dev):
+        copy = remote(src, dst, ssem, rsem, dev)
+        copy.start()
+        started.append((None, copy))
+
+    def send_if(cond, src, dst, ssem, rsem, dev):
+        copy = remote(src, dst, ssem, rsem, dev)
+
+        @pl.when(cond)
+        def _():
+            copy.start()
+        started.append((cond, copy))
+
+    def got(ref, ssem, rsem):
+        remote(ref, ref, ssem, rsem, (xe, t, r)).wait_recv()
+
+    for d in range(1, nt):
+        to = lax.rem(t + d, nt)
+        send(req_ref, ag.at[t], ag_s.at[d], ag_r.at[t], (xe, to, r))
+    for d in range(1, nx):
+        send(meta_ref, meta.at[xe], me_s.at[d], me_r.at[xe], (xe ^ d, t, r))
+    loads = [
+        pltpu.make_async_copy(up_hbm, up, lsem.at[0]),
+        pltpu.make_async_copy(down_hbm, down, lsem.at[1]),
+        pltpu.make_async_copy(tin_hbm, tin, lsem.at[2]),
+    ]
+    for load in loads:
+        load.start()
+    meta[xe] = meta_ref[...]
+
+    for d in (3, 1, 2, 0):
+        tx = xe ^ d
+        own = tx == t
+
+        @pl.when(jnp.logical_not(own))
+        def _():
+            got(ag.at[tx], ag_s.at[0], ag_r.at[tx])
+        for flip in (0, 1):
+            if d == 0 and flip == 0:
+                continue
+            ss, rs = x_s.at[2 * d + flip], x_r.at[xe, r]
+            dev = (tx, t, r ^ flip)
+            send_if(own, req_ref, xin.at[xe, r], ss, rs, dev)
+            send_if(jnp.logical_not(own), ag.at[tx], xin.at[xe, r], ss, rs, dev)
+
+    is_own = xe == t
+
+    @pl.when(is_own)
+    def _():
+        xin[xe, r] = req_ref[...]
+
+    @pl.when(jnp.logical_not(is_own))
+    def _():
+        xin[xe, r] = ag[xe]
+
+    for d in range(1, nx):
+        got(meta.at[xe ^ d], me_s.at[0], me_r.at[xe ^ d])
+    for d in range(nx):
+        for flip in range(nr):
+            if d == 0 and flip == 0:
+                continue
+            slot = (xe ^ d, r ^ flip)
+            got(xin.at[slot], x_s.at[0], x_r.at[slot])
+    for b in range(nx):
+        for k in range(nr):
+            xs[b, :, k * feat:(k + 1) * feat] = xin[b, k]
+    info = [meta[b].T for b in range(nx)]
+
+    def column(c, j):
+        return jnp.concatenate([info[b][c * sub:(c + 1) * sub, j:j + 1] for b in range(nx)], axis=0)
+
+    loads[0].wait()
+    quarter = xe
+    near = (1, 2)
+    for c in range(CHUNKS):
+        rows = xs[:, c * sub:(c + 1) * sub, :].reshape(nx * sub, nr * feat)
+        ids = (column(c, 0), column(c, 1))
+        for h in range(2):
+            picked = [jnp.zeros((nx * sub, hcols), F32)] * 2
+            for e in range(experts):
+                part = jnp.dot(rows, up[e, :, h * hcols:(h + 1) * hcols], preferred_element_type=F32)
+                picked = [jnp.where(ids[k] == float(e), part, picked[k]) for k in range(2)]
+            for k in range(2):
+                hp[c, h, :, k * sub:(k + 1) * sub, :] = picked[k].astype(BF16).reshape(nx, sub, hcols)
+            fa, fb = near[h], near[1 - h]
+            for i, q in enumerate((quarter ^ fa ^ fb, quarter ^ fa)):
+                send(hp.at[c, h, q], r1.at[c, h, i], s1_s.at[c, h, i], s1_r.at[c, h, i],
+                     (xe ^ fa, t, r))
+
+    def reduce_first(c, h):
+        fa, fb = near[h], near[1 - h]
+        got(r1.at[c, h, 0], s1_s.at[c, h, 0], s1_r.at[c, h, 0])
+        s2[c, h] = (hp[c, h, quarter ^ fb].astype(F32) + r1[c, h, 0].astype(F32)).astype(BF16)
+        send(s2.at[c, h], r2.at[c, h], s2_s.at[c, h], s2_r.at[c, h], (xe ^ fb, t, r))
+
+    def reduce_second(c, h):
+        fa, fb = near[h], near[1 - h]
+        got(r1.at[c, h, 1], s1_s.at[c, h, 1], s1_r.at[c, h, 1])
+        got(r2.at[c, h], s2_s.at[c, h], s2_r.at[c, h])
+        total = (hp[c, h, quarter].astype(F32) + r1[c, h, 1].astype(F32)) + r2[c, h].astype(F32)
+        hid[c, h, quarter] = jnp.maximum(total, 0.0).astype(BF16)
+        for i, f in enumerate((fb, fa)):
+            send(hid.at[c, h, quarter], hid.at[c, h, quarter], h_s.at[c, h, i],
+                 h_r.at[c, h, quarter], (xe ^ f, t, r))
+
+    def forward(c, h):
+        fa, fb = near[h], near[1 - h]
+        q = quarter ^ fb
+        got(hid.at[c, h, q], h_s.at[c, h, 2], h_r.at[c, h, q])
+        send(hid.at[c, h, q], hid.at[c, h, q], h_s.at[c, h, 2], h_r.at[c, h, q], (xe ^ fa, t, r))
+
+    def collect(c, h):
+        fa, fb = near[h], near[1 - h]
+        for q in (quarter ^ fa, quarter ^ fa ^ fb):
+            got(hid.at[c, h, q], h_s.at[c, h, 2], h_r.at[c, h, q])
+
+    def down_chunk(c):
+        ids = (column(c, 0), column(c, 1))
+        gates = (column(c, 2), column(c, 3))
+        total = jnp.zeros((nx * sub, nr * feat), F32)
+        for e in range(experts):
+            hit = (ids[0] == float(e), ids[1] == float(e))
+            weight = jnp.where(hit[0], gates[0], 0.0) + jnp.where(hit[1], gates[1], 0.0)
+            part = None
+            for h in range(2):
+                values = [hid[c, h, :, k * sub:(k + 1) * sub, :].reshape(nx * sub, hcols)
+                          for k in range(2)]
+                chosen = jnp.where(hit[0], values[0], jnp.where(hit[1], values[1], jnp.zeros_like(values[1])))
+                one = lax.dot_general(chosen, down[e, :, h * hcols:(h + 1) * hcols],
+                                      (((1,), (1,)), ((), ())), preferred_element_type=F32)
+                part = one if part is None else part + one
+            total = total + weight * part
+        low, high = total[:, :feat], total[:, feat:]
+        mine[c] = jnp.where(r == 0, low, high).reshape(nx, sub, feat)
+        dsend0[c] = jnp.where(r == 0, high, low).astype(BF16).reshape(nx, sub, feat)
+        send(dsend0.at[c], drecv0.at[c], p_s.at[c], p_r.at[c], (xe, t, 1 - r))
+
+    here = t == xe
+
+    def pair_chunk(c):
+        got(drecv0.at[c], p_s.at[c], p_r.at[c])
+        dsend[c] = (mine[c] + drecv0[c].astype(F32)).astype(BF16)
+        for b in range(nx):
+            self_copy = jnp.logical_and(here, xe == b)
+
+            @pl.when(self_copy)
+            def _():
+                drecv[c, t] = dsend[c, b]
+            send_if(jnp.logical_not(self_copy), dsend.at[c, b], drecv.at[c, t], d_s.at[c, b],
+                    d_r.at[c, t], (b, xe, r))
+
+    def mixed_chunk(c):
+        for src in range(nt):
+            @pl.when(jnp.logical_not(jnp.logical_and(here, t == src)))
+            def _():
+                got(drecv.at[c, src], d_s.at[c, 0], d_r.at[c, src])
+        total = drecv[c, 0].astype(F32)
+        for src in range(1, nt):
+            total = total + drecv[c, src].astype(F32)
+        value = total.astype(BF16)
+        mixed_ref[c * sub:(c + 1) * sub, :] = value
+        part = jnp.dot(value, tin[...], preferred_element_type=F32).astype(BF16)
+        each = tok // (nt * nr)
+        per = sub // each
+        fsend[c * per:(c + 1) * per] = part.reshape(per, each, part.shape[1])
+
+    todo = [(c, h) for c in range(CHUNKS) for h in range(2)]
+    for c in range(CHUNKS):
+        for h in range(2):
+            reduce_first(c, h)
+        for h in range(2):
+            reduce_second(c, h)
+    loads[1].wait()
+    loads[2].wait()
+    for c in range(CHUNKS):
+        for h in range(2):
+            forward(c, h)
+    for c in range(CHUNKS):
+        for h in range(2):
+            collect(c, h)
+        down_chunk(c)
+    for c in range(CHUNKS):
+        pair_chunk(c)
+    for c in range(CHUNKS):
+        mixed_chunk(c)
+    me = t * nr + r
+    for d in range(1, nt * nr):
+        to = me ^ d
+        send(fsend.at[to], frecv.at[me], f_s.at[d], f_r.at[me],
+             (xe, lax.div(to, nr), lax.rem(to, nr)))
+    pre = fsend[me].astype(F32)
+    for d in range(1, nt * nr):
+        frm = me ^ d
+        got(frecv.at[frm], f_s.at[d], f_r.at[frm])
+        pre = pre + frecv[frm].astype(F32)
+    active = jnp.maximum(pre + bias_ref[...], 0.0)
+    outs = []
+    for j in range(tasks):
+        outs.append(jnp.sum(active[:, j * th:(j + 1) * th] * tout_ref[j:j + 1, :], axis=1, keepdims=True))
+    each = pre.shape[0]
+    lane = lax.broadcasted_iota(jnp.int32, (each, 128), 1)
+    logits = jnp.zeros((each, 128), F32)
+    for j in range(tasks):
+        logits = jnp.where(lane == j, outs[j], logits)
+    flipped = logits.T[:tasks, :] + ob_ref[...]
+    scores_ref[...] = jax.nn.sigmoid(flipped)
+    for cond, copy in started:
+        if cond is None:
+            copy.wait_send()
+        else:
+            @pl.when(cond)
+            def _(copy=copy):
+                copy.wait_send()
+
+
+def stay_device(requests, expert_ids, gate_values, w_up, w_down, tower_in, tower_bias, tower_out,
+                out_bias):
+    nx, nt, nr = lax.axis_size("expert"), lax.axis_size("tensor"), lax.axis_size("rep")
+    experts, _, hid_cols = w_up.shape
+    tok, feat = requests.shape
+    tasks, th = tower_out.shape
+    hcols = hid_cols // 2
+    sub = tok // CHUNKS
+    each = tok // (nt * nr)
+    dims = (nx, nt, nr, experts, tok, feat, hcols, tasks, th)
+    meta = jnp.concatenate(
+        [expert_ids.T.astype(F32), gate_values.T, jnp.zeros((4, tok), F32)], axis=0)
+    vmem = pl.BlockSpec(memory_space=pltpu.VMEM)
+    hbm = pl.BlockSpec(memory_space=pl.ANY)
+    dma = pltpu.SemaphoreType.DMA
+    C = CHUNKS
+    scratch = [
+        pltpu.VMEM(w_up.shape, BF16), pltpu.VMEM(w_down.shape, BF16),
+        pltpu.VMEM(tower_in.shape, BF16),
+        pltpu.VMEM((nt, tok, feat), BF16), pltpu.VMEM((nx, 8, tok), F32),
+        pltpu.VMEM((nx, nr, tok, feat), BF16), pltpu.VMEM((nx, tok, nr * feat), BF16),
+        pltpu.VMEM((C, 2, nx, 2 * sub, hcols), BF16),
+        pltpu.VMEM((C, 2, 2, 2 * sub, hcols), BF16),
+        pltpu.VMEM((C, 2, 2 * sub, hcols), BF16), pltpu.VMEM((C, 2, 2 * sub, hcols), BF16),
+        pltpu.VMEM((C, 2, nx, 2 * sub, hcols), BF16),
+        pltpu.VMEM((C, nx, sub, feat), F32), pltpu.VMEM((C, nx, sub, feat), BF16),
+        pltpu.VMEM((C, nx, sub, feat), BF16), pltpu.VMEM((C, nx, sub, feat), BF16),
+        pltpu.VMEM((C, nt, sub, feat), BF16),
+        pltpu.VMEM((nt * nr, each, tasks * th), BF16), pltpu.VMEM((nt * nr, each, tasks * th), BF16),
+        dma((3,)), dma((nt,)), dma((nt,)), dma((nx,)), dma((nx,)), dma((2 * nx,)), dma((nx, nr)),
+        dma((C, 2, 2)), dma((C, 2, 2)), dma((C, 2)), dma((C, 2)), dma((C, 2, 3)), dma((C, 2, nx)),
+        dma((C,)), dma((C,)), dma((C, nx)), dma((C, nt)), dma((nt * nr,)), dma((nt * nr,)),
+    ]
+    return pl.pallas_call(
+        functools.partial(stay_kernel, dims),
+        out_shape=(jax.ShapeDtypeStruct((tok, feat), BF16), jax.ShapeDtypeStruct((tasks, each), F32)),
+        in_specs=[vmem, vmem, hbm, hbm, hbm, vmem, vmem, vmem],
+        out_specs=(vmem, vmem),
+        scratch_shapes=scratch,
+        compiler_params=pltpu.CompilerParams(has_side_effects=True, vmem_limit_bytes=48 << 20),
+        name="stay",
+    )(requests, meta, w_up, w_down, tower_in, tower_bias[None, :], tower_out, out_bias[:, None])
+
+
+def weights_stay(mesh):
+    return mesh.shape["expert"] == 4 and mesh.shape["tensor"] == 4 and mesh.shape["rep"] == 2
 
 
 def tower_head(pre, tower_bias, tower_out, out_bias):
@@ -76,6 +364,7 @@
         P(),
     )
     out_specs = (P("expert", ("tensor", "rep")), P(None, ("expert", "tensor", "rep")))
+    body = stay_device if weights_stay(mesh) else per_device
     return jax.shard_map(
-        per_device, mesh=mesh, in_specs=in_specs, out_specs=out_specs, check_vma=False
-    )
+        body, mesh=mesh, in_specs=in_specs, out_specs=out_specs, check_vma=False
+    )

time: 199 us -> 91.6 us (0.46)
  blocking collectives: 95.8 us -> 0 us
  Pallas kernels: 0 us -> 80.5 us
  waiting for transfers between devices: 65.8 us -> 0 us
  between operations: 14.2 us -> 0.67 us
  matrix products: 7.42 us -> 0 us
  starting transfers between devices: 3.68 us -> 0 us
    pallas_call x0 -> x1, Pallas kernels: none -> 80.5 us  [stay_device(): pl.pallas_call(functools.partial(stay_kernel, dims), out_shape=(jax.Shape...]
    all_to_all x3 -> x0, blocking collectives: 79.4 us -> none  [the longest x1 30.1 us: per_device(): lax.all_to_all(w_up, 'expert', split_axis=0, concat_axis=1, tiled=True)]
    unnamed x3 -> x0, waiting for transfers between devices: 32.7 us -> none
    reduce_scatter x1 -> x0, waiting for transfers between devices: 27.9 us -> none  [per_device(): lax.psum_scatter(jnp.dot(mixed, tower_in, preferred_element_type=jnp.floa...]
    all_gather x1 -> x0, blocking collectives: 16.4 us -> none  [per_device(): full_rows = lax.all_gather(requests, ('tensor', 'rep'), axis=1, tiled=True)]
    dot_general x5 -> x0, matrix products: 7.42 us -> none  [the longest x1 5.47 us: per_device(): jnp.einsum('sech,edh->secd', hidden, serve_down, preferred_element_type=j...]
    all_to_all x1 -> x0, waiting for transfers between devices: 5.18 us -> none  [per_device(): lax.all_to_all(expert_out, 'expert', split_axis=0, concat_axis=0, tiled=T...]
    all_to_all x1 -> x0, starting transfers between devices: 3.64 us -> none  [per_device(): lax.all_to_all(expert_out, 'expert', split_axis=0, concat_axis=0, tiled=T...]
  transfers between devices with their start and end apart: 3 -> 0, of which waited for: 3 -> 0; matrix products, arithmetic and copies ran while one was open for 0% -> 0% of each run, Pallas kernels for 0% -> 0%
where the time goes in v1:
time: 91.6 us; the launch traced here: 91.3 us
  Pallas kernels  80.5 us (88%)
  local copies, waits for them, and re-layouts  8.67 us (9%)
  other arithmetic  1.43 us (2%)
    pallas_call x1, Pallas kernels, stay_device(): pl.pallas_call(functools.partial(stay_kernel, dims), out_shape=(jax.Shape...  80.5 us
    unnamed x10, local copies, waits for them, and re-layouts  6.44 us

profile of v1, /device:TPU:0, one launch (start us, length us, event | category | flops | bytes accessed | tf_op | source)
XLA Modules:
  0.0 91.3 jit_solution(4792007909780307387)
XLA Ops:
  0.6 0.1 pad.2.clone
  0.7 0.7 convert_bitcast_fusion
  1.4 0.7 copy.12.ob_ref
  2.1 0.7 maximum_maximum_fusion.meta_ref
  2.9 0.7 broadcast_in_dim.10.bias_ref
  3.6 0.9 copy.11.req_ref
  4.5 0.0 copy-start
  4.5 1.7 %copy-done = bf16[4,384,768]{2,1,0:T(8,128)(2,1)S(1)} copy-done((bf16[4,384,768]{2,1,0:T(8,128)(2,1)S(1)}, bf16[4,384,768]{2,1,0:T(8,128)(2,1)}, u32[]{:S(2)}) %copy-start) | copy-done | bytes 2359320
  6.1 0.0 copy-start.1
  6.1 1.7 %copy-done.1 = bf16[4,384,768]{2,1,0:T(8,128)(2,1)S(1)} copy-done((bf16[4,384,768]{2,1,0:T(8,128)(2,1)S(1)}, bf16[4,384,768]{2,1,0:T(8,128)(2,1)}, u32[]{:S(2)}) %copy-start.1) | copy-done | bytes 2359320
  7.8 0.0 copy-start.2
  7.8 1.0 %copy-done.2 = bf16[192,768]{1,0:T(8,128)(2,1)S(1)} copy-done((bf16[192,768]{1,0:T(8,128)(2,1)S(1)}, bf16[192,768]{1,0:T(8,128)(2,1)}, u32[]{:S(2)}) %copy-start.2) | copy-done | bytes 294936
  8.8 0.0 copy-start.3
  8.8 0.7 copy-done.3
  9.5 80.5 %stay.1 = (bf16[128,192]{1,0:T(8,128)(2,1)S(1)}, f32[3,16]{1,0:T(4,128)S(1)}) custom-call(bf16[128,192]{1,0:T(8,128)(2,1)S(1)} %copy.11.req_ref, f32[8,128]{1,0:T(8,128)S(1)} %maximum_maximum_fusion.meta_ref, bf16[4,384,768]{2,1,0:T(8,128)(2,1)S(1)} %copy-done, bf16[4,384,768]{2,1,0:T(8,128)(2,1)S(1)} %copy-done.1, bf16[192,768]{1,0:T(8,128)(2,1)S(1)} %copy-done.2, ...), custom_call_target="tpu_custom_call" | custom-call | tf_op jit(solution)/shard_map/stay/pallas_call | solution.py:280
  90.0 0.7 copy.13
  90.7 0.6 copy.15
  (1 shorter events, 0.0 us)
Async XLA Ops:
  4.5 1.7 %copy-start = (bf16[4,384,768]{2,1,0:T(8,128)(2,1)S(1)}, bf16[4,384,768]{2,1,0:T(8,128)(2,1)}, u32[]{:S(2)}) copy-start(bf16[4,384,768]{2,1,0:T(8,128)(2,1)} %up_hbm.1) | copy-start | bytes 7077892
  6.1 1.7 %copy-start.1 = (bf16[4,384,768]{2,1,0:T(8,128)(2,1)S(1)}, bf16[4,384,768]{2,1,0:T(8,128)(2,1)}, u32[]{:S(2)}) copy-start(bf16[4,384,768]{2,1,0:T(8,128)(2,1)} %down_hbm.1) | copy-start | bytes 7077892
  7.8 1.0 %copy-start.2 = (bf16[192,768]{1,0:T(8,128)(2,1)S(1)}, bf16[192,768]{1,0:T(8,128)(2,1)}, u32[]{:S(2)}) copy-start(bf16[192,768]{1,0:T(8,128)(2,1)} %tin_hbm.1) | copy-start | bytes 884740
  8.8 0.7 copy-start.3

commit v2 on v1

--- a/solution.py
+++ b/solution.py
@@ -7,16 +7,16 @@
 from jax.sharding import PartitionSpec as P
 
 MESH = pl.DeviceIdType.MESH
-CHUNKS = 2
+CHUNKS = 4
 F32 = jnp.float32
 BF16 = jnp.bfloat16
 
 
 def stay_kernel(
-    dims, req_ref, meta_ref, up_hbm, down_hbm, tin_hbm, bias_ref, tout_ref, ob_ref,
+    dims, req_hbm, ids_hbm, gates_hbm, up_hbm, down_hbm, tin_hbm, bias_hbm, tout_hbm, ob_ref,
     mixed_ref, scores_ref,
-    up, down, tin, ag, meta, xin, xs, hp, r1, s2, r2, hid, mine, dsend0, drecv0, dsend, drecv,
-    fsend, frecv, lsem, ag_s, ag_r, me_s, me_r, x_s, x_r, s1_s, s1_r, s2_s, s2_r, h_s, h_r,
+    req_ref, ids_ref, gates_ref, bias_ref, tout_ref, up, down, tin, ag, meta_ref, meta, xin, xs, hp, r1, s2, r2, hid, mine, dsend0, drecv0, dsend, drecv,
+    fsend, frecv, mixed_rows, lsem, ag_s, ag_r, me_s, me_r, x_s, x_r, s1_s, s1_r, s2_s, s2_r, h_s, h_r,
     p_s, p_r, d_s, d_r, f_s, f_r,
 ):
     nx, nt, nr, experts, tok, feat, hcols, tasks, th = dims
@@ -45,18 +45,60 @@
     def got(ref, ssem, rsem):
         remote(ref, ref, ssem, rsem, (xe, t, r)).wait_recv()
 
+    first = [
+        pltpu.make_async_copy(req_hbm, req_ref, lsem.at[3]),
+        pltpu.make_async_copy(ids_hbm, ids_ref, lsem.at[4]),
+        pltpu.make_async_copy(gates_hbm, gates_ref, lsem.at[5]),
+    ]
+    loads = [
+        pltpu.make_async_copy(up_hbm, up, lsem.at[0]),
+        pltpu.make_async_copy(down_hbm, down, lsem.at[1]),
+        pltpu.make_async_copy(tin_hbm, tin, lsem.at[2]),
+        pltpu.make_async_copy(bias_hbm, bias_ref, lsem.at[6]),
+        pltpu.make_async_copy(tout_hbm, tout_ref, lsem.at[7]),
+    ]
+    for load in first + loads:
+        load.start()
+    here = t == xe
+    barrier = pltpu.get_barrier_semaphore()
+
+    def greet(dev):
+        pl.semaphore_signal(barrier, inc=1, device_id=dev, device_id_type=MESH)
+
+    me = t * nr + r
+    for d in range(1, nt * nr):
+        other = me ^ d
+        greet((xe, lax.div(other, nr), lax.rem(other, nr)))
+    for d in range(1, nx):
+        for flip in range(nr):
+            greet((xe ^ d, t, r ^ flip))
+    for b in range(nx):
+        @pl.when(jnp.logical_not(jnp.logical_and(here, xe == b)))
+        def _():
+            greet((b, xe, r))
+
+        @pl.when(jnp.logical_not(jnp.logical_and(here, t == b)))
+        def _():
+            greet((t, b, r))
+    for load in first:
+        load.wait()
+    meta_ref[...] = jnp.concatenate(
+        [ids_ref[...].astype(F32), gates_ref[...], jnp.zeros((4, tok), F32)], axis=0)
+    greeted = (nt * nr - 1) + (nx - 1) * nr + 2 * nx
+
+    @pl.when(here)
+    def _():
+        pl.semaphore_wait(barrier, greeted - 2)
+
+    @pl.when(jnp.logical_not(here))
+    def _():
+        pl.semaphore_wait(barrier, greeted)
+
     for d in range(1, nt):
         to = lax.rem(t + d, nt)
         send(req_ref, ag.at[t], ag_s.at[d], ag_r.at[t], (xe, to, r))
     for d in range(1, nx):
         send(meta_ref, meta.at[xe], me_s.at[d], me_r.at[xe], (xe ^ d, t, r))
-    loads = [
-        pltpu.make_async_copy(up_hbm, up, lsem.at[0]),
-        pltpu.make_async_copy(down_hbm, down, lsem.at[1]),
-        pltpu.make_async_copy(tin_hbm, tin, lsem.at[2]),
-    ]
-    for load in loads:
-        load.start()
     meta[xe] = meta_ref[...]
 
     for d in (3, 1, 2, 0):
@@ -94,7 +136,7 @@
             got(xin.at[slot], x_s.at[0], x_r.at[slot])
     for b in range(nx):
         for k in range(nr):
-            xs[b, :, k * feat:(k + 1) * feat] = xin[b, k]
+            xs[b, :, k * feat:(k + 1) * feat] = xin[b, k].T
     info = [meta[b].T for b in range(nx)]
 
     def column(c, j):
@@ -103,7 +145,7 @@
     loads[0].wait()
     quarter = xe
     near = (1, 2)
-    for c in range(CHUNKS):
+    def up_chunk(c):
         rows = xs[:, c * sub:(c + 1) * sub, :].reshape(nx * sub, nr * feat)
         ids = (column(c, 0), column(c, 1))
         for h in range(2):
@@ -166,8 +208,6 @@
         dsend0[c] = jnp.where(r == 0, high, low).astype(BF16).reshape(nx, sub, feat)
         send(dsend0.at[c], drecv0.at[c], p_s.at[c], p_r.at[c], (xe, t, 1 - r))
 
-    here = t == xe
-
     def pair_chunk(c):
         got(drecv0.at[c], p_s.at[c], p_r.at[c])
         dsend[c] = (mine[c] + drecv0[c].astype(F32)).astype(BF16)
@@ -189,42 +229,43 @@
         for src in range(1, nt):
             total = total + drecv[c, src].astype(F32)
         value = total.astype(BF16)
-        mixed_ref[c * sub:(c + 1) * sub, :] = value
+        mixed_rows[c * sub:(c + 1) * sub, :] = value
         part = jnp.dot(value, tin[...], preferred_element_type=F32).astype(BF16)
         each = tok // (nt * nr)
         per = sub // each
         fsend[c * per:(c + 1) * per] = part.reshape(per, each, part.shape[1])
-
-    todo = [(c, h) for c in range(CHUNKS) for h in range(2)]
-    for c in range(CHUNKS):
-        for h in range(2):
-            reduce_first(c, h)
-        for h in range(2):
-            reduce_second(c, h)
-    loads[1].wait()
-    loads[2].wait()
-    for c in range(CHUNKS):
-        for h in range(2):
-            forward(c, h)
-    for c in range(CHUNKS):
-        for h in range(2):
-            collect(c, h)
-        down_chunk(c)
-    for c in range(CHUNKS):
-        pair_chunk(c)
-    for c in range(CHUNKS):
-        mixed_chunk(c)
-    me = t * nr + r
-    for d in range(1, nt * nr):
-        to = me ^ d
-        send(fsend.at[to], frecv.at[me], f_s.at[d], f_r.at[me],
-             (xe, lax.div(to, nr), lax.rem(to, nr)))
+        for to in range(c * per, (c + 1) * per):
+            send_if(me != to, fsend.at[to], frecv.at[me], f_s.at[to], f_r.at[me],
+                    (xe, to // nr, to % nr))
+
+    def both(stage, c):
+        if 0 <= c < CHUNKS:
+            for h in range(2):
+                stage(c, h)
+
+    def one(stage, c):
+        if 0 <= c < CHUNKS:
+            stage(c)
+
+    for i in range(CHUNKS + 8):
+        if i == 5:
+            for load in loads[1:]:
+                load.wait()
+        both(forward, i - 4)
+        both(reduce_second, i - 3)
+        both(reduce_first, i - 2)
+        one(up_chunk, i)
+        both(collect, i - 5)
+        one(down_chunk, i - 5)
+        one(pair_chunk, i - 6)
+        one(mixed_chunk, i - 7)
+    mixed_ref[...] = mixed_rows[...].T
     pre = fsend[me].astype(F32)
     for d in range(1, nt * nr):
         frm = me ^ d
-        got(frecv.at[frm], f_s.at[d], f_r.at[frm])
+        got(frecv.at[frm], f_s.at[0], f_r.at[frm])
         pre = pre + frecv[frm].astype(F32)
-    active = jnp.maximum(pre + bias_ref[...], 0.0)
+    active = jnp.maximum(pre + bias_ref[...].reshape(1, tasks * th), 0.0)
     outs = []
     for j in range(tasks):
         outs.append(jnp.sum(active[:, j * th:(j + 1) * th] * tout_ref[j:j + 1, :], axis=1, keepdims=True))
@@ -232,9 +273,8 @@
     lane = lax.broadcasted_iota(jnp.int32, (each, 128), 1)
     logits = jnp.zeros((each, 128), F32)
     for j in range(tasks):
-        logits = jnp.where(lane == j, outs[j], logits)
-    flipped = logits.T[:tasks, :] + ob_ref[...]
-    scores_ref[...] = jax.nn.sigmoid(flipped)
+        logits = jnp.where(lane == j, outs[j] + ob_ref[j], logits)
+    scores_ref[...] = jax.nn.sigmoid(logits.T[:tasks, :])
     for cond, copy in started:
         if cond is None:
             copy.wait_send()
@@ -254,17 +294,18 @@
     sub = tok // CHUNKS
     each = tok // (nt * nr)
     dims = (nx, nt, nr, experts, tok, feat, hcols, tasks, th)
-    meta = jnp.concatenate(
-        [expert_ids.T.astype(F32), gate_values.T, jnp.zeros((4, tok), F32)], axis=0)
     vmem = pl.BlockSpec(memory_space=pltpu.VMEM)
-    hbm = pl.BlockSpec(memory_space=pl.ANY)
+    hbm = pl.BlockSpec(memory_space=pltpu.HBM)
+    smem = pl.BlockSpec(memory_space=pltpu.SMEM)
     dma = pltpu.SemaphoreType.DMA
     C = CHUNKS
     scratch = [
+        pltpu.VMEM((feat, tok), BF16), pltpu.VMEM((2, tok), jnp.int32), pltpu.VMEM((2, tok), F32),
+        pltpu.VMEM(tower_bias.shape, F32), pltpu.VMEM(tower_out.shape, F32),
         pltpu.VMEM(w_up.shape, BF16), pltpu.VMEM(w_down.shape, BF16),
         pltpu.VMEM(tower_in.shape, BF16),
-        pltpu.VMEM((nt, tok, feat), BF16), pltpu.VMEM((nx, 8, tok), F32),
-        pltpu.VMEM((nx, nr, tok, feat), BF16), pltpu.VMEM((nx, tok, nr * feat), BF16),
+        pltpu.VMEM((nt, feat, tok), BF16), pltpu.VMEM((8, tok), F32), pltpu.VMEM((nx, 8, tok), F32),
+        pltpu.VMEM((nx, nr, feat, tok), BF16), pltpu.VMEM((nx, tok, nr * feat), BF16),
         pltpu.VMEM((C, 2, nx, 2 * sub, hcols), BF16),
         pltpu.VMEM((C, 2, 2, 2 * sub, hcols), BF16),
         pltpu.VMEM((C, 2, 2 * sub, hcols), BF16), pltpu.VMEM((C, 2, 2 * sub, hcols), BF16),
@@ -273,19 +314,22 @@
         pltpu.VMEM((C, nx, sub, feat), BF16), pltpu.VMEM((C, nx, sub, feat), BF16),
         pltpu.VMEM((C, nt, sub, feat), BF16),
         pltpu.VMEM((nt * nr, each, tasks * th), BF16), pltpu.VMEM((nt * nr, each, tasks * th), BF16),
-        dma((3,)), dma((nt,)), dma((nt,)), dma((nx,)), dma((nx,)), dma((2 * nx,)), dma((nx, nr)),
+        pltpu.VMEM((tok, feat), BF16),
+        dma((8,)), dma((nt,)), dma((nt,)), dma((nx,)), dma((nx,)), dma((2 * nx,)), dma((nx, nr)),
         dma((C, 2, 2)), dma((C, 2, 2)), dma((C, 2)), dma((C, 2)), dma((C, 2, 3)), dma((C, 2, nx)),
         dma((C,)), dma((C,)), dma((C, nx)), dma((C, nt)), dma((nt * nr,)), dma((nt * nr,)),
     ]
-    return pl.pallas_call(
+    mixed, scores = pl.pallas_call(
         functools.partial(stay_kernel, dims),
-        out_shape=(jax.ShapeDtypeStruct((tok, feat), BF16), jax.ShapeDtypeStruct((tasks, each), F32)),
-        in_specs=[vmem, vmem, hbm, hbm, hbm, vmem, vmem, vmem],
+        out_shape=(jax.ShapeDtypeStruct((feat, tok), BF16), jax.ShapeDtypeStruct((tasks, each), F32)),
+        in_specs=[hbm] * 8 + [smem],
         out_specs=(vmem, vmem),
         scratch_shapes=scratch,
-        compiler_params=pltpu.CompilerParams(has_side_effects=True, vmem_limit_bytes=48 << 20),
+        compiler_params=pltpu.CompilerParams(
+            has_side_effects=True, collective_id=0, vmem_limit_bytes=60 << 20),
         name="stay",
-    )(requests, meta, w_up, w_down, tower_in, tower_bias[None, :], tower_out, out_bias[:, None])
+    )(requests.T, expert_ids.T, gate_values.T, w_up, w_down, tower_in, tower_bias, tower_out, out_bias)
+    return mixed.T, scores
 
 
 def weights_stay(mesh):

time: 91.6 us -> 71.3 us (0.78)
  Pallas kernels: 80.5 us -> 67.8 us
  local copies, waits for them, and re-layouts: 8.67 us -> 2.66 us
  other arithmetic: 1.43 us -> 0 us
    pallas_call x1, Pallas kernels: 80.5 us -> 67.8 us  [stay_device(): pl.pallas_call(functools.partial(stay_kernel, dims), out_shape=(jax.Shape...]
    unnamed x10 -> x2, local copies, waits for them, and re-layouts: 6.44 us -> 2.66 us
    broadcast_in_dim x3 -> x0, local copies, waits for them, and re-layouts: 1.43 us -> none  [the longest x1 0.74 us: stay_device(): out_bias[:, None]]
where the time goes in v2:
time: 71.3 us; the launch traced here: 71.1 us
  Pallas kernels  67.8 us (95%)
  local copies, waits for them, and re-layouts  2.66 us (4%)
    pallas_call x1, Pallas kernels, stay_device(): pl.pallas_call(functools.partial(stay_kernel, dims), out_shape=(jax.Shape...  67.8 us
    unnamed x2, local copies, waits for them, and re-layouts  2.66 us

profile of v2, /device:TPU:0, one launch (start us, length us, event | category | flops | bytes accessed | tf_op | source)
XLA Modules:
  0.0 71.1 jit_solution(2517197679732280544)
XLA Ops:
  0.6 67.8 %stay.1 = (bf16[192,128]{1,0:T(8,128)(2,1)}, f32[3,16]{1,0:T(4,128)}) custom-call(bf16[192,128]{1,0:T(8,128)(2,1)} %bitcast.4, s32[2,128]{1,0:T(2,128)} %bitcast.6, f32[2,128]{1,0:T(2,128)} %bitcast.7, bf16[4,384,768]{2,1,0:T(8,128)(2,1)} %up_hbm.1, bf16[4,384,768]{2,1,0:T(8,128)(2,1)} %down_hbm.1, bf16[192,768]{1,0:T(8,128)(2,1)} %tin_hbm.1, f32[768]{0:T(1024)} %bias_hbm.1, ...), custom_call_target="tpu_custom_call" | custom-call | tf_op jit(solution)/shard_map/stay/pallas_call | solution.py:322
  68.4 1.4 %copy.13 = bf16[128,192]{0,1:T(8,128)(2,1)} copy(bf16[128,192]{0,1:T(8,128)(2,1)} %bitcast.5) | data formatting | bytes 98304
  69.8 1.2 %copy.14 = f32[3,16]{1,0:T(4,128)} copy(f32[3,16]{1,0:T(4,128)} %get-tuple-element.9) | data formatting | bytes 384
